TPU v7x, 32 devices: a whole 2x2x4 slice. The times are simulated.
32 devices in a mesh: heads: 4 (over y, core), batch: 8 (over z, x).
Axes of the slice: x: 2, y: 2, z: 4, core: 2. Of those that a mesh axis runs over, the one named last changes fastest.
Arguments:
- queries: bfloat16 [64, 4096], P('batch', 'heads'), may hold values from -6 to 6
- keys_new: bfloat16 [64, 4096], P('batch', 'heads'), may hold values from -6 to 6
- values_new: bfloat16 [64, 4096], P('batch', 'heads'), may hold values from -6 to 6
- out_gate: bfloat16 [64, 4096], P('batch', 'heads'), may hold values from -6 to 6
- decay_logit: float32 [64, 32], P('batch', 'heads'), may hold values from -6 to 6
- beta_logit: float32 [64, 32], P('batch', 'heads'), may hold values from -6 to 6
- decay_rate: float32 [32], P('heads'), may hold values from 0.05 to 2
- state: float32 [64, 32, 128, 128], P('batch', 'heads'), may hold values from -0.6 to 0.6
- norm_gain: float32 [128], replicated, may hold values from 0.1 to 1.9
- out_proj: bfloat16 [4096, 4096], P('heads'), may hold values from -0.09375 to 0.09375
- residual: bfloat16 [64, 4096], P('batch'), may hold values from -40 to 40, as said below
- final_gain: float32 [4096], replicated, may hold values from 0.1 to 1.9
- value_weight: float32 [4096], replicated, may hold values from -0.09375 to 0.09375
- lm_head: bfloat16 [4096, 4096], P(None, ('heads', 'batch')), may hold values from -15 to 15
- sampled: int32 [64], replicated, may hold values from 0 to 4095
Outputs:
- logprob: float32 [64], P('batch')
- value: float32 [64], P('batch')
Inputs may be any that keep to these rules, and one draw needn't show every extreme that they name: The residual stream's entries have scales that differ by row and by column (up to tenfold each), so neither rows nor columns share one magnitude.
All inputs are finite; a program needn't handle non-finite values.
Results may differ from a plain program's by a relative error of at most 0.0013.
Values may be sent and summed in bfloat16 or wider, within the bound.
A program may use at most 64 MiB of HBM per device.

v0:
```python
import jax
import jax.numpy as jnp
from jax import lax
from jax.sharding import PartitionSpec as P

epsilon = 1e-06


def joined(part, axis, combine):
    gathered = jax.tree.map(lambda a: lax.all_gather(a, axis), part)

    def take(source):
        return jax.tree.map(lambda a: lax.dynamic_index_in_dim(a, source, 0, False), gathered)

    return lax.fori_loop(
        1, lax.axis_size(axis), lambda source, state: combine(state, take(source)), take(0)
    )


def head_outputs(
    queries, keys_new, values_new, out_gate, decay_logit, beta_logit, decay_rate, state, norm_gain
):
    rows_here, heads_here = decay_logit.shape
    query_f = queries.astype(jnp.float32).reshape(rows_here, heads_here, -1)
    key_f = keys_new.astype(jnp.float32).reshape(rows_here, heads_here, -1)
    value_f = values_new.astype(jnp.float32).reshape(rows_here, heads_here, -1)
    gate_f = out_gate.astype(jnp.float32).reshape(rows_here, heads_here, -1)
    key_size = query_f.shape[2]
    query_n = query_f / jnp.sqrt(jnp.sum(query_f * query_f, axis=2, keepdims=True) + epsilon)
    query_n = query_n * key_size ** (-0.5)
    key_n = key_f / jnp.sqrt(jnp.sum(key_f * key_f, axis=2, keepdims=True) + epsilon)
    decay = jnp.exp(-decay_rate[None, :] * jax.nn.softplus(decay_logit))
    strength = jax.nn.sigmoid(beta_logit)
    state_query = jnp.einsum("bhk,bhkv->bhv", query_n, state, precision=lax.Precision.HIGHEST)
    state_key = jnp.einsum("bhk,bhkv->bhv", key_n, state, precision=lax.Precision.HIGHEST)
    intersection = jnp.sum(query_n * key_n, axis=2, keepdims=True)
    written = value_f - decay[..., None] * state_key
    output = decay[..., None] * state_query + strength[..., None] * intersection * written
    normed = output / jnp.sqrt(jnp.mean(output * output, axis=2, keepdims=True) + epsilon)
    result = normed * norm_gain * jax.nn.silu(gate_f)
    return result.reshape(rows_here, -1).astype(jnp.bfloat16)


def merge_stats(earlier, later):
    top = jnp.maximum(earlier[0], later[0])
    total = earlier[1] * jnp.exp(earlier[0] - top) + later[1] * jnp.exp(later[0] - top)
    return (top, total, earlier[2] + later[2])


def per_device(
    queries,
    keys_new,
    values_new,
    out_gate,
    decay_logit,
    beta_logit,
    decay_rate,
    state,
    norm_gain,
    out_proj,
    residual,
    final_gain,
    value_weight,
    lm_head,
    sampled,
):
    headout = head_outputs(
        queries,
        keys_new,
        values_new,
        out_gate,
        decay_logit,
        beta_logit,
        decay_rate,
        state,
        norm_gain,
    )
    partial_out = jnp.dot(headout, out_proj, preferred_element_type=jnp.float32)
    rows_own = residual.shape[0]
    attn = lax.psum(partial_out, "heads")
    hsum = residual.astype(jnp.float32) + attn
    rstd = 1.0 / jnp.sqrt(jnp.mean(hsum * hsum, axis=1) + epsilon)
    value = rstd * jnp.sum(hsum * final_gain * value_weight, axis=1)
    normed = (hsum * rstd[:, None] * final_gain).astype(jnp.bfloat16)
    logits = jnp.dot(
        lax.all_gather(normed, "batch", axis=0, tiled=True),
        lm_head,
        preferred_element_type=jnp.float32,
    )
    vocab_own = lm_head.shape[1]
    vocab_first = lax.axis_index(("heads", "batch")) * vocab_own
    local_ids = sampled - vocab_first
    columns = lax.broadcasted_iota(jnp.int32, logits.shape, 1)
    chosen = jnp.sum(jnp.where(columns == local_ids[:, None], logits, 0.0), axis=1)
    local_top = jnp.max(logits, axis=1)
    local_total = jnp.sum(jnp.exp(logits - local_top[:, None]), axis=1)
    top, total, chosen_all = joined(
        (local_top, local_total, chosen), ("heads", "batch"), merge_stats
    )
    every_logprob = chosen_all - (top + jnp.log(total))
    logprob = lax.dynamic_slice_in_dim(
        every_logprob, lax.axis_index("batch") * rows_own, rows_own, 0
    )
    return (logprob, value)


def solution(mesh):
    placed = (
        P("batch", "heads"),
        P("batch", "heads"),
        P("batch", "heads"),
        P("batch", "heads"),
        P("batch", "heads"),
        P("batch", "heads"),
        P("heads"),
        P("batch", "heads", None, None),
        P(),
        P("heads", None),
        P("batch", None),
        P(),
        P(),
        P(None, ("heads", "batch")),
        P(),
    )
    return jax.shard_map(
        per_device, mesh=mesh, in_specs=placed, out_specs=(P("batch"), P("batch")), check_vma=False
    )
```

profile of v0, /device:TPU:0, one launch (start us, length us, event | category | flops | bytes accessed | tf_op | source)
XLA Modules:
  0.0 143.0 jit_solution(5027682328408560421)
XLA Ops:
  7.2 0.0 copy-start
  7.2 0.0 all-reduce.6.cloned.1.call-start
  7.2 0.0 copy-start.1
  7.2 1.0 fusion.7
  8.2 1.1 fusion.9
  9.3 0.9 fusion.22
  10.2 0.0 copy-start.7
  10.3 0.0 copy-start.10
  10.3 0.0 copy-start.8
  10.3 0.0 copy-start.3
  10.3 0.0 copy-start.5
  10.3 0.0 copy-start.9
  10.3 5.3 %fusion.16 = f32[8,8,1,128]{3,2,1,0:T(1,128)S(1)} fusion(f32[8,8,128,128]{3,2,1,0:T(8,128)} %param.24, f32[8,8,128,1]{2,0,1,3:T(8,128)S(1)} %get-tuple-element.209), kind=kOutput, calls=%fused_computation.32 | convolution fusion | flops 12582912 | bytes 4259840 | tf_op jit(solution)/shard_map/bhk,bhkv->bhv/dot_general | solution.py:35
  15.6 0.0 copy-done.1
  15.6 3.7 %fusion.18 = f32[8,8,1,128]{3,2,1,0:T(1,128)S(1)} fusion(f32[8,8,128,128]{3,2,1,0:T(8,128)S(1)} %copy-done.1, f32[8,8,128,1]{2,0,1,3:T(8,128)S(1)} %get-tuple-element.207), kind=kOutput, calls=%fused_computation.34 | convolution fusion | flops 12582912 | bytes 4259840 | tf_op jit(solution)/shard_map/bhk,bhkv->bhv/dot_general | solution.py:34
  19.3 0.0 copy-done.7
  19.3 0.1 copy.20
  19.4 0.0 copy-done.10
  19.4 0.0 copy-done.8
  19.4 0.1 copy.19
  19.5 0.0 copy-done.3
  19.5 0.2 multiply_reduce_fusion.2
  19.7 0.0 copy-done.5
  19.7 0.0 copy-done.9
  19.7 0.0 copy-start.11
  19.7 0.0 copy-start.2
  19.7 0.0 copy-start.4
  19.7 0.0 copy-start.6
  19.7 5.3 %fusion.23 = f32[8,4096]{1,0:T(8,128)} fusion(bf16[1024,4096]{1,0:T(8,128)(2,1)} %param.26, bf16[8,1024]{1,0:T(8,128)(2,1)S(1)} %copy-done.5, f32[128]{0:T(128)S(1)} %copy-done.9, f32[8,8]{0,1:T(8,128)S(1)} %add_sqrt_fusion, f32[8,8,1,128]{3,2,1,0:T(1,128)S(1)} %fusion.16, f32[8,8,1,128]{3,2,1,0:T(1,128)S(1)} %fusion.18, bf16[8,1024]{1,0:T(8,128)(2,1)S(1)} %copy-done.3, ...), kind=kOutput, calls=%fused_computation.44 | convolution fusion | flops 67231744 | bytes 8619264 | tf_op jit(solution)/shard_map/dot_general | solution.py:78
  25.0 0.0 all-reduce.6.cloned.1.call-update
  25.1 0.0 copy-done.11
  25.1 34.6 %all-reduce.6.cloned.1.call-done = f32[8,4096]{1,0:T(8,128)} async-done(((f32[8,4096]{1,0:T(8,128)}), f32[8,4096]{1,0:T(8,128)}) %all-reduce.6.cloned.1.call-update) | async-done | bytes 131088 | tf_op jit(solution)/shard_map/psum | solution.py:80
  59.7 0.0 copy-done.2
  59.7 0.0 copy-done.4
  59.7 0.0 copy-done.6
  59.7 1.1 multiply_reduce_fusion
  60.8 0.5 fusion.32
  61.4 1.0 multiply_convert_fusion
  62.4 31.4 %all_gather.21 = bf16[64,4096]{1,0:T(8,128)(2,1)S(1)} all-gather(bf16[8,4096]{1,0:T(8,128)(2,1)S(1)} %multiply_convert_fusion), channel_id=1, replica_groups=mesh['heads'=4,'batch'=8] {'batch'}, dimensions={0}, use_global_device_ids=true | all-gather | bytes 589824 | tf_op jit(solution)/shard_map/all_gather | solution.py:86
  93.7 0.0 copy-done
  93.7 0.4 fusion.35
  94.2 0.2 select_reduce_fusion
  94.4 0.3 dynamic-update-slice
  94.7 0.3 dynamic-update-slice.2
  94.9 0.3 dynamic-update-slice.1
  95.2 38.7 %all-reduce.3 = (f32[2048]{0:T(1024)S(1)}, f32[2048]{0:T(1024)S(1)}, f32[2048]{0:T(1024)S(1)}) all-reduce(f32[2048]{0:T(1024)S(1)} %dynamic-update-slice, f32[2048]{0:T(1024)S(1)} %dynamic-update-slice.1, f32[2048]{0:T(1024)S(1)} %dynamic-update-slice.2), channel_id=2, replica_groups=mesh['heads'=4,'batch'=8] {'heads','batch'}, use_global_device_ids=true, to_apply=%add | all-reduce | flops 6144 | bytes 49152
  133.8 0.1 reshape.81
  133.9 0.1 reshape.82
  134.0 0.1 reshape.83
  134.1 1.4 %while.19 = (s32[]{:T(128)}, f32[64]{0:T(128)S(1)}, f32[64]{0:T(128)S(1)}, f32[64]{0:T(128)S(1)}, f32[32,64]{1,0:T(8,128)S(1)}, /*index=5*/f32[32,64]{1,0:T(8,12...) while((s32[]{:T(128)}, f32[64]{0:T(128)S(1)}, f32[64]{0:T(128)S(1)}, f32[64]{0:T(128)S(1)}, ...), condition=%wide.region_10.11_spmd, body=%wide.region_9.10_spmd.sunk | while | flops 453 | bytes 2451 | solution.py:15
  135.5 0.6 dynamic_slice.46
  (44 shorter events, 0.9 us)
Async XLA Ops:
  7.2 86.6 %copy-start = (bf16[4096,128]{1,0:T(8,128)(2,1)S(1)}, bf16[4096,128]{1,0:T(8,128)(2,1)}, u32[]{:S(2)}) copy-start(bf16[4096,128]{1,0:T(8,128)(2,1)} %param.30) | copy-start | bytes 3145732
  7.2 52.6 %all-reduce.6.cloned.1.call-start = ((), (), s32[]{:S(2)}) async-start(), calls=%async_computation | async-start | bytes 262144 | tf_op jit(solution)/shard_map/psum | solution.py:80
  7.2 8.4 %copy-start.1 = (f32[8,8,128,128]{3,2,1,0:T(8,128)S(1)}, f32[8,8,128,128]{3,2,1,0:T(8,128)}, u32[]{:S(2)}) copy-start(f32[8,8,128,128]{3,2,1,0:T(8,128)} %param.24) | copy-start | bytes 12582916
  10.2 9.1 %copy-start.7 = (f32[8,8]{1,0:T(8,128)S(1)}, f32[8,8]{1,0:T(8,128)}, u32[]{:S(2)}) copy-start(f32[8,8]{1,0:T(8,128)} %param.22) | copy-start | bytes 772
  10.3 9.1 %copy-start.10 = (f32[8]{0:T(128)S(1)}, f32[8]{0:T(128)}, u32[]{:S(2)}) copy-start(f32[8]{0:T(128)} %param.23) | copy-start | bytes 100
  10.3 9.1 %copy-start.8 = (f32[8,8]{1,0:T(8,128)S(1)}, f32[8,8]{1,0:T(8,128)}, u32[]{:S(2)}) copy-start(f32[8,8]{1,0:T(8,128)} %param.21) | copy-start | bytes 772
  10.3 9.2 %copy-start.3 = (bf16[8,1024]{1,0:T(8,128)(2,1)S(1)}, bf16[8,1024]{1,0:T(8,128)(2,1)}, u32[]{:S(2)}) copy-start(bf16[8,1024]{1,0:T(8,128)(2,1)} %param.19) | copy-start | bytes 49156
  10.3 9.4 %copy-start.5 = (bf16[8,1024]{1,0:T(8,128)(2,1)S(1)}, bf16[8,1024]{1,0:T(8,128)(2,1)}, u32[]{:S(2)}) copy-start(bf16[8,1024]{1,0:T(8,128)(2,1)} %param.20) | copy-start | bytes 49156
  10.3 9.4 %copy-start.9 = (f32[128]{0:T(128)S(1)}, f32[128]{0:T(128)}, u32[]{:S(2)}) copy-start(f32[128]{0:T(128)} %param.25) | copy-start | bytes 1540
  19.7 5.4 %copy-start.11 = (s32[64]{0:T(128)S(1)}, s32[64]{0:T(128)}, u32[]{:S(2)}) copy-start(s32[64]{0:T(128)} %param.31) | copy-start | bytes 772
  19.7 40.0 %copy-start.2 = (bf16[8,4096]{1,0:T(8,128)(2,1)S(1)}, bf16[8,4096]{1,0:T(8,128)(2,1)}, u32[]{:S(2)}) copy-start(bf16[8,4096]{1,0:T(8,128)(2,1)} %param.27) | copy-start | bytes 196612
  19.7 40.0 %copy-start.4 = (f32[4096]{0:T(1024)S(1)}, f32[4096]{0:T(1024)}, u32[]{:S(2)}) copy-start(f32[4096]{0:T(1024)} %param.28) | copy-start | bytes 49156
  19.7 40.0 %copy-start.6 = (f32[4096]{0:T(1024)S(1)}, f32[4096]{0:T(1024)}, u32[]{:S(2)}) copy-start(f32[4096]{0:T(1024)} %param.29) | copy-start | bytes 49156
Sparse Core Ops, SparseCore 0:
  25.2 34.4 all-reduce.5
where the time goes:
time: 144 us; the launch traced here: 143 us
  blocking collectives  70.1 us (49%)
  waiting for transfers between devices  34.6 us (24%)
  matrix products  14.7 us (10%)
  between operations  14.2 us (10%)
  other arithmetic  6.89 us (5%)
  local copies, waits for them, and re-layouts  1.82 us (1%)
    unnamed x1, blocking collectives  38.7 us
    psum x1, waiting for transfers between devices, per_device(): attn = lax.psum(partial_out, 'heads')  34.6 us
    all_gather x1, blocking collectives, per_device(): lax.all_gather(normed, 'batch', axis=0, tiled=True)  31.4 us
    dot_general x1, matrix products, head_outputs(): jnp.einsum('bhk,bhkv->bhv', key_n, state, precision=lax.Precision.HIGHEST)  5.31 us
    dot_general x1, matrix products, per_device(): partial_out = jnp.dot(headout, out_proj, preferred_element_type=jnp.float32)  5.31 us
    dot_general x1, matrix products, head_outputs(): jnp.einsum('bhk,bhkv->bhv', query_n, state, precision=lax.Precision.HIGHEST)  3.66 us
  transfers between devices with their start and end apart: 1, of which 1 were waited for; matrix products, arithmetic and copies ran while one was open for 0% of the time, Pallas kernels for 0%

commit v1 on v0

v1 whole, which is shorter than its diff:
```python
import functools

import jax
import jax.numpy as jnp
from jax import lax
from jax.experimental import pallas as pl
from jax.experimental.pallas import tpu as pltpu
from jax.sharding import PartitionSpec as P

MESH = pl.DeviceIdType.MESH
epsilon = 1e-06
f32 = jnp.float32
bf16 = jnp.bfloat16


def kernel(
    n_h,
    n_b,
    q_hbm,
    k_hbm,
    v_hbm,
    g_hbm,
    dl_hbm,
    bl_hbm,
    dr_hbm,
    state_hbm,
    ng_hbm,
    proj_hbm,
    res_hbm,
    fg_hbm,
    vw_hbm,
    lm_hbm,
    sampled_hbm,
    logprob_ref,
    value_ref,
    q_v,
    k_v,
    v_v,
    g_v,
    dl_v,
    bl_v,
    dr_v,
    st_v,
    ng_v,
    wp_v,
    res_v,
    fg_v,
    vw_v,
    lm_v,
    sampled_v,
    ho_v,
    part_v,
    rs_v,
    ssend_v,
    stat_v,
    gx_v,
    fx_v,
    small_sem,
    st_sem,
    wp_sem,
    rs_send,
    rs_recv,
    stat_send,
    stat_recv,
    g_send,
    g_recv,
    f_send,
    f_recv,
):
    n_all = n_h * n_b
    my_h = lax.axis_index("heads")
    my_b = lax.axis_index("batch")
    me = my_h * n_b + my_b
    my_y, my_c = my_h // 2, my_h % 2
    n_y = n_h // 2
    rows, width = q_v.shape
    heads_here = st_v.shape[1]
    size = st_v.shape[2]
    cols = res_v.shape[1]
    batch = sampled_v.shape[1]

    def peer(step):
        return ((my_y + 1 + step // 2) % n_y) * 2 + (my_c + step + 1) % 2

    early = [
        (q_hbm, q_v),
        (k_hbm, k_v),
        (v_hbm, v_v),
        (g_hbm, g_v),
        (dl_hbm, dl_v),
        (bl_hbm, bl_v),
        (dr_hbm, dr_v),
        (ng_hbm, ng_v),
    ]
    own_cols = pl.ds(pl.multiple_of(my_h * cols, cols), cols)
    late = [
        (res_hbm.at[:, own_cols], res_v),
        (fg_hbm.at[:, own_cols], fg_v),
        (vw_hbm.at[:, own_cols], vw_v),
        (lm_hbm, lm_v),
        (sampled_hbm, sampled_v),
    ]
    loads = [
        pltpu.make_async_copy(src, dst, small_sem.at[i])
        for i, (src, dst) in enumerate(early + late)
    ]
    n_early = len(early)
    for copy in loads[:n_early]:
        copy.start()
    st_loads = [
        pltpu.make_async_copy(state_hbm.at[:, h], st_v.at[:, h], st_sem.at[h])
        for h in range(heads_here)
    ]
    for copy in st_loads:
        copy.start()
    wp_loads = []
    for s in range(n_h):
        at = pl.ds(pl.multiple_of(peer(s) * cols, cols), cols)
        wp_loads.append(pltpu.make_async_copy(proj_hbm.at[:, at], wp_v.at[s], wp_sem.at[s]))
    for copy in wp_loads:
        copy.start()
    for copy in loads[n_early:]:
        copy.start()

    barrier = pltpu.get_barrier_semaphore()

    def greet(o, carry):
        other = (me + o) % n_all
        pl.semaphore_signal(
            barrier, inc=1, device_id=(other // n_b, other % n_b), device_id_type=MESH
        )
        return carry

    lax.fori_loop(1, n_all, greet, 0)

    for copy in loads[:n_early]:
        copy.wait()

    x = dl_v[...]
    softplus = jnp.maximum(x, 0.0) + jnp.log1p(jnp.exp(-jnp.abs(x)))
    decay_all = jnp.exp(-dr_v[...] * softplus)
    strength_all = 1.0 / (1.0 + jnp.exp(-bl_v[...]))
    head_lane = lax.broadcasted_iota(jnp.int32, x.shape, 1)
    norm_gain = ng_v[...]

    def head(h, carry):
        pltpu.make_async_copy(state_hbm.at[:, h], st_v.at[:, h], st_sem.at[h]).wait()
        at = pl.ds(pl.multiple_of(h * size, size), size)
        q = q_v[:, at].astype(f32)
        k = k_v[:, at].astype(f32)
        v = v_v[:, at].astype(f32)
        g = g_v[:, at].astype(f32)
        qn = q / jnp.sqrt(jnp.sum(q * q, axis=1, keepdims=True) + epsilon) * size ** (-0.5)
        kn = k / jnp.sqrt(jnp.sum(k * k, axis=1, keepdims=True) + epsilon)
        cross = jnp.sum(qn * kn, axis=1, keepdims=True)
        here = head_lane == h
        decay = jnp.sum(jnp.where(here, decay_all, 0.0), axis=1, keepdims=True)
        strength = jnp.sum(jnp.where(here, strength_all, 0.0), axis=1, keepdims=True)
        qt = qn.T
        kt = kn.T
        sq, sk = [], []
        for b in range(rows):
            s = st_v[b, h]
            sq.append(jnp.sum(qt[:, b : b + 1] * s, axis=0, keepdims=True))
            sk.append(jnp.sum(kt[:, b : b + 1] * s, axis=0, keepdims=True))
        sq = jnp.concatenate(sq, axis=0)
        sk = jnp.concatenate(sk, axis=0)
        o = decay * sq + strength * cross * (v - decay * sk)
        o = o / jnp.sqrt(jnp.mean(o * o, axis=1, keepdims=True) + epsilon)
        ho_v[:, at] = o * norm_gain * (g / (1.0 + jnp.exp(-g)))
        return carry

    lax.fori_loop(0, heads_here, head, 0)
    headout = ho_v[...].astype(bf16)

    rs_copies = []
    own = None
    for s in range(n_h):
        wp_loads[s].wait()
        part = jnp.dot(headout, wp_v[s], preferred_element_type=f32)
        if s == n_h - 1:
            own = part
            break
        part_v[s] = part
        if s == 0:
            pl.semaphore_wait(barrier, n_all - 1)
        copy = pltpu.make_async_remote_copy(
            src_ref=part_v.at[s],
            dst_ref=rs_v.at[s],
            send_sem=rs_send.at[s],
            recv_sem=rs_recv.at[s],
            device_id=(peer(s), my_b),
            device_id_type=MESH,
        )
        copy.start()
        rs_copies.append(copy)

    for copy in loads[n_early:]:
        copy.wait()
    hsum = res_v[...].astype(f32) + own
    for s in range(n_h - 1):
        rs_copies[s].wait_recv()
        hsum = hsum + rs_v[s]

    gain = fg_v[...]
    square = jnp.sum(hsum * hsum, axis=1, keepdims=True)
    weighed = jnp.sum(hsum * gain * vw_v[...], axis=1, keepdims=True)
    lane = lax.broadcasted_iota(jnp.int32, ssend_v.shape, 1)
    half = ssend_v.shape[1] // 2
    total = jnp.where(lane < half, square, weighed)
    ssend_v[...] = total
    stat_copies = []
    for s in range(n_h - 1):
        copy = pltpu.make_async_remote_copy(
            src_ref=ssend_v,
            dst_ref=stat_v.at[s],
            send_sem=stat_send.at[s],
            recv_sem=stat_recv.at[s],
            device_id=(peer(s), my_b),
            device_id_type=MESH,
        )
        copy.start()
        stat_copies.append(copy)
    for s in range(n_h - 1):
        stat_copies[s].wait_recv()
        total = total + stat_v[s]
    width_all = cols * n_h
    rstd = 1.0 / jnp.sqrt(total[:, :1] / width_all + epsilon)
    gx_v[me] = (hsum * rstd * gain).astype(bf16)

    def spread(o, carry):
        other = (me + o) % n_all
        other_h = other // n_b
        pltpu.make_async_remote_copy(
            src_ref=gx_v.at[me],
            dst_ref=gx_v.at[me],
            send_sem=g_send,
            recv_sem=g_recv.at[(my_h - other_h + n_h) % n_h],
            device_id=(other_h, other % n_b),
            device_id_type=MESH,
        ).start()
        return carry

    lax.fori_loop(1, n_all, spread, 0)

    value = rstd * total[:, half : half + 1]
    row_of = lax.broadcasted_iota(jnp.int32, ssend_v.shape, 0)
    value_ref[...] = jnp.sum(jnp.where(row_of == lane, value, 0.0), axis=0, keepdims=True)[:, :rows]

    logits = None
    for r in range(n_h):
        other_h = (my_h + r) % n_h
        arrived = gx_v.at[pl.ds(0, n_b if r else n_b - 1)]
        pltpu.make_async_copy(arrived, arrived, g_recv.at[r]).wait()
        block = jnp.concatenate(
            [gx_v[other_h * n_b + b].astype(f32) for b in range(n_b)], axis=0
        ).astype(bf16)
        at = pl.ds(pl.multiple_of(other_h * cols, cols), cols)
        term = jnp.dot(block, lm_v[at, :], preferred_element_type=f32)
        logits = term if logits is None else logits + term

    logits = logits.T
    vocab_own = lm_v.shape[1]
    ids = lax.broadcasted_iota(jnp.int32, logits.shape, 0) + me * vocab_own
    chosen = jnp.sum(jnp.where(ids == sampled_v[...], logits, 0.0), axis=0, keepdims=True)
    top = jnp.max(logits, axis=0, keepdims=True)
    mass = jnp.sum(jnp.exp(logits - top), axis=0, keepdims=True)
    fx_v[me, 0:1, :batch] = top + jnp.log(mass)
    fx_v[me, 1:2, :batch] = chosen

    def tell(o, carry):
        other = (me + o) % n_all
        pltpu.make_async_remote_copy(
            src_ref=fx_v.at[me],
            dst_ref=fx_v.at[me],
            send_sem=f_send,
            recv_sem=f_recv,
            device_id=(other // n_b, other % n_b),
            device_id_type=MESH,
        ).start()
        return carry

    lax.fori_loop(1, n_all, tell, 0)
    arrived = fx_v.at[pl.ds(0, n_all - 1)]
    pltpu.make_async_copy(arrived, arrived, f_recv).wait()

    both = fx_v[...]
    lse = both[:, 0, :]
    picked = jnp.sum(both[:, 1, :], axis=0, keepdims=True)
    best = jnp.max(lse, axis=0, keepdims=True)
    every = picked - (best + jnp.log(jnp.sum(jnp.exp(lse - best), axis=0, keepdims=True)))
    lanes = every.shape[1]
    pick = lax.broadcasted_iota(jnp.int32, (rows, lanes), 1) == (
        lax.broadcasted_iota(jnp.int32, (rows, lanes), 0) + my_b * rows
    )
    column = jnp.sum(jnp.where(pick, every, 0.0), axis=1, keepdims=True)
    logprob_ref[...] = jnp.sum(jnp.where(row_of == lane, column, 0.0), axis=0, keepdims=True)[
        :, :rows
    ]

    for s in range(n_h - 1):
        rs_copies[s].wait_send()
        stat_copies[s].wait_send()
    sent = gx_v.at[pl.ds(0, n_all - 1)]
    pltpu.make_async_copy(sent, sent, g_send).wait()
    sent = fx_v.at[pl.ds(0, n_all - 1)]
    pltpu.make_async_copy(sent, sent, f_send).wait()


def solution(mesh):
    n_h, n_b = mesh.shape["heads"], mesh.shape["batch"]

    def per_device(
        queries,
        keys_new,
        values_new,
        out_gate,
        decay_logit,
        beta_logit,
        decay_rate,
        state,
        norm_gain,
        out_proj,
        residual,
        final_gain,
        value_weight,
        lm_head,
        sampled,
    ):
        rows, width = queries.shape
        cols = out_proj.shape[1] // n_h
        n_all = n_h * n_b
        batch = sampled.shape[0]
        heads_here = state.shape[1]
        padded = max(batch, 128)
        like = lambda a: pltpu.VMEM(a.shape, a.dtype)
        decay_rate, norm_gain, final_gain, value_weight, sampled = (
            a.reshape(1, -1) for a in (decay_rate, norm_gain, final_gain, value_weight, sampled)
        )
        scratch = [
            like(queries),
            like(keys_new),
            like(values_new),
            like(out_gate),
            like(decay_logit),
            like(beta_logit),
            like(decay_rate),
            like(state),
            like(norm_gain),
            pltpu.VMEM((n_h, width, cols), bf16),
            pltpu.VMEM((rows, cols), bf16),
            pltpu.VMEM((1, cols), f32),
            pltpu.VMEM((1, cols), f32),
            like(lm_head),
            like(sampled),
            pltpu.VMEM((rows, width), f32),
            pltpu.VMEM((n_h - 1, rows, cols), f32),
            pltpu.VMEM((n_h - 1, rows, cols), f32),
            pltpu.VMEM((rows, 128), f32),
            pltpu.VMEM((n_h - 1, rows, 128), f32),
            pltpu.VMEM((n_all, rows, cols), bf16),
            pltpu.VMEM((n_all, 2, padded), f32),
            pltpu.SemaphoreType.DMA((13,)),
            pltpu.SemaphoreType.DMA((heads_here,)),
            pltpu.SemaphoreType.DMA((n_h,)),
            pltpu.SemaphoreType.DMA((n_h - 1,)),
            pltpu.SemaphoreType.DMA((n_h - 1,)),
            pltpu.SemaphoreType.DMA((n_h - 1,)),
            pltpu.SemaphoreType.DMA((n_h - 1,)),
            pltpu.SemaphoreType.DMA,
            pltpu.SemaphoreType.DMA((n_h,)),
            pltpu.SemaphoreType.DMA,
            pltpu.SemaphoreType.DMA,
        ]
        logprob, value = pl.pallas_call(
            functools.partial(kernel, n_h, n_b),
            out_shape=(
                jax.ShapeDtypeStruct((1, rows), f32),
                jax.ShapeDtypeStruct((1, rows), f32),
            ),
            in_specs=[pl.BlockSpec(memory_space=pl.ANY)] * 15,
            out_specs=(
                pl.BlockSpec(memory_space=pltpu.VMEM),
                pl.BlockSpec(memory_space=pltpu.VMEM),
            ),
            scratch_shapes=scratch,
            compiler_params=pltpu.CompilerParams(
                collective_id=0, has_side_effects=True, vmem_limit_bytes=48 * 1024 * 1024
            ),
        )(
            queries,
            keys_new,
            values_new,
            out_gate,
            decay_logit,
            beta_logit,
            decay_rate,
            state,
            norm_gain,
            out_proj,
            residual,
            final_gain,
            value_weight,
            lm_head,
            sampled,
        )
        return logprob.reshape(rows), value.reshape(rows)

    placed = (
        P("batch", "heads"),
        P("batch", "heads"),
        P("batch", "heads"),
        P("batch", "heads"),
        P("batch", "heads"),
        P("batch", "heads"),
        P("heads"),
        P("batch", "heads", None, None),
        P(),
        P("heads", None),
        P("batch", None),
        P(),
        P(),
        P(None, ("heads", "batch")),
        P(),
    )
    return jax.shard_map(
        per_device, mesh=mesh, in_specs=placed, out_specs=(P("batch"), P("batch")), check_vma=False
    )
```

time: 144 us -> 49.6 us (0.34)
  blocking collectives: 70.1 us -> 0 us
  Pallas kernels: 0 us -> 35.2 us
  waiting for transfers between devices: 34.6 us -> 0 us
  matrix products: 14.7 us -> 0 us
  between operations: 14.2 us -> 0.67 us
  local copies, waits for them, and re-layouts: 1.82 us -> 12.9 us
  other arithmetic: 6.89 us -> 0 us
    unnamed x1 -> x0, blocking collectives: 38.7 us -> none
    pallas_call x0 -> x1, Pallas kernels: none -> 35.2 us  [per_device(): pl.pallas_call(functools.partial(kernel, n_h, n_b), out_shape=(jax.ShapeD...]
    psum x1 -> x0, waiting for transfers between devices: 34.6 us -> none  [per_device(): attn = lax.psum(partial_out, 'heads')]
    all_gather x1 -> x0, blocking collectives: 31.4 us -> none  [per_device(): lax.all_gather(normed, 'batch', axis=0, tiled=True)]
    dot_general x4 -> x0, matrix products: 14.7 us -> none  [the longest x1 5.31 us: head_outputs(): jnp.einsum('bhk,bhkv->bhv', key_n, state, precision=lax.Precision.HIGHEST)]
    unnamed x31 -> x30, local copies, waits for them, and re-layouts: 0.94 us -> 12.9 us
    reduce_sum x5 -> x0, other arithmetic: 3.54 us -> none  [the longest x1 1.12 us: head_outputs(): jnp.sum(key_f * key_f, axis=2, keepdims=True) + epsilon]
    mul x3 -> x0, other arithmetic: 1.44 us -> none  [the longest x1 0.9 us: head_outputs(): query_n = query_n * key_size ** (-0.5)]
  transfers between devices with their start and end apart: 1 -> 0, of which waited for: 1 -> 0; matrix products, arithmetic and copies ran while one was open for 0% -> 0% of each run, Pallas kernels for 0% -> 0%
where the time goes in v1:
time: 49.6 us; the launch traced here: 48.8 us
  Pallas kernels  35.2 us (71%)
  local copies, waits for them, and re-layouts  12.9 us (26%)
  between operations  0.67 us (1%)
    pallas_call x1, Pallas kernels, per_device(): pl.pallas_call(functools.partial(kernel, n_h, n_b), out_shape=(jax.ShapeD...  35.2 us
    unnamed x30, local copies, waits for them, and re-layouts  12.9 us

profile of v1, /device:TPU:0, one launch (start us, length us, event | category | flops | bytes accessed | tf_op | source)
XLA Modules:
  0.0 48.8 jit_solution(1538102369251229250)
XLA Ops:
  0.6 0.0 copy-start
  0.6 2.2 %copy-done = f32[8,8,128,128]{3,2,1,0:T(8,128)S(1)} copy-done((f32[8,8,128,128]{3,2,1,0:T(8,128)S(1)}, f32[8,8,128,128]{3,2,1,0:T(8,128)}, u32[]{:S(2)}) %copy-start) | copy-done | bytes 4194328
  2.8 0.0 copy-start.1
  2.8 1.2 %copy-done.1 = bf16[4096,128]{1,0:T(8,128)(2,1)S(1)} copy-done((bf16[4096,128]{1,0:T(8,128)(2,1)S(1)}, bf16[4096,128]{1,0:T(8,128)(2,1)}, u32[]{:S(2)}) %copy-start.1) | copy-done | bytes 1048600
  4.1 0.0 copy-start.2
  4.1 0.8 %copy-done.2 = bf16[8,4096]{1,0:T(8,128)(2,1)S(1)} copy-done((bf16[8,4096]{1,0:T(8,128)(2,1)S(1)}, bf16[8,4096]{1,0:T(8,128)(2,1)}, u32[]{:S(2)}) %copy-start.2) | copy-done | bytes 65560
  4.9 0.0 copy-start.3
  4.9 0.7 %copy-done.3 = bf16[8,1024]{1,0:T(8,128)(2,1)S(1)} copy-done((bf16[8,1024]{1,0:T(8,128)(2,1)S(1)}, bf16[8,1024]{1,0:T(8,128)(2,1)}, u32[]{:S(2)}) %copy-start.3) | copy-done | bytes 16408
  5.6 0.0 copy-start.4
  5.6 0.7 %copy-done.4 = bf16[8,1024]{1,0:T(8,128)(2,1)S(1)} copy-done((bf16[8,1024]{1,0:T(8,128)(2,1)S(1)}, bf16[8,1024]{1,0:T(8,128)(2,1)}, u32[]{:S(2)}) %copy-start.4) | copy-done | bytes 16408
  6.3 0.0 copy-start.5
  6.3 0.7 %copy-done.5 = bf16[8,1024]{1,0:T(8,128)(2,1)S(1)} copy-done((bf16[8,1024]{1,0:T(8,128)(2,1)S(1)}, bf16[8,1024]{1,0:T(8,128)(2,1)}, u32[]{:S(2)}) %copy-start.5) | copy-done | bytes 16408
  7.0 0.0 copy-start.6
  7.0 0.7 %copy-done.6 = bf16[8,1024]{1,0:T(8,128)(2,1)S(1)} copy-done((bf16[8,1024]{1,0:T(8,128)(2,1)S(1)}, bf16[8,1024]{1,0:T(8,128)(2,1)}, u32[]{:S(2)}) %copy-start.6) | copy-done | bytes 16408
  7.8 0.0 copy-start.7
  7.8 0.7 %copy-done.7 = f32[4096]{0:T(1024)S(1)} copy-done((f32[4096]{0:T(1024)S(1)}, f32[4096]{0:T(1024)}, u32[]{:S(2)}) %copy-start.7) | copy-done | bytes 16408
  8.5 0.0 copy-start.8
  8.5 0.7 %copy-done.8 = f32[4096]{0:T(1024)S(1)} copy-done((f32[4096]{0:T(1024)S(1)}, f32[4096]{0:T(1024)}, u32[]{:S(2)}) %copy-start.8) | copy-done | bytes 16408
  9.2 0.0 copy-start.9
  9.2 0.7 %copy-done.9 = f32[8,8]{1,0:T(8,128)S(1)} copy-done((f32[8,8]{1,0:T(8,128)S(1)}, f32[8,8]{1,0:T(8,128)}, u32[]{:S(2)}) %copy-start.9) | copy-done | bytes 280
  9.9 0.0 copy-start.10
  9.9 0.7 %copy-done.10 = f32[8,8]{1,0:T(8,128)S(1)} copy-done((f32[8,8]{1,0:T(8,128)S(1)}, f32[8,8]{1,0:T(8,128)}, u32[]{:S(2)}) %copy-start.10) | copy-done | bytes 280
  10.6 0.0 copy-start.11
  10.6 0.7 %copy-done.11 = f32[8]{0:T(128)S(1)} copy-done((f32[8]{0:T(128)S(1)}, f32[8]{0:T(128)}, u32[]{:S(2)}) %copy-start.11) | copy-done | bytes 56
  11.2 0.0 copy-start.12
  11.2 0.7 %copy-done.12 = f32[128]{0:T(128)S(1)} copy-done((f32[128]{0:T(128)S(1)}, f32[128]{0:T(128)}, u32[]{:S(2)}) %copy-start.12) | copy-done | bytes 536
  11.9 0.0 copy-start.13
  11.9 0.7 %copy-done.13 = s32[64]{0:T(128)S(1)} copy-done((s32[64]{0:T(128)S(1)}, s32[64]{0:T(128)}, u32[]{:S(2)}) %copy-start.13) | copy-done | bytes 280
  12.5 35.2 %shard_map.158 = (f32[1,8]{1,0:T(1,128)S(1)}, f32[1,8]{1,0:T(1,128)S(1)}) custom-call(bf16[8,1024]{1,0:T(8,128)(2,1)S(1)} %copy-done.3, bf16[8,1024]{1,0:T(8,128)(2,1)S(1)} %copy-done.4, bf16[8,1024]{1,0:T(8,128)(2,1)S(1)} %copy-done.5, bf16[8,1024]{1,0:T(8,128)(2,1)S(1)} %copy-done.6, f32[8,8]{1,0:T(8,128)S(1)} %copy-done.9, f32[8,8]{1,0:T(8,128)S(1)} %copy-done.10, ...), custom_call_target="tpu_custom_call" | custom-call | tf_op jit(solution)/shard_map/pallas_call | solution.py:375
  47.7 0.5 %copy.19 = f32[8]{0:T(128)} copy(f32[8]{0:T(128)S(1)} %bitcast.13) | data formatting | bytes 64
  48.3 0.5 %copy.20 = f32[8]{0:T(128)} copy(f32[8]{0:T(128)S(1)} %bitcast.12) | data formatting | bytes 64
Async XLA Ops:
  0.6 2.2 %copy-start = (f32[8,8,128,128]{3,2,1,0:T(8,128)S(1)}, f32[8,8,128,128]{3,2,1,0:T(8,128)}, u32[]{:S(2)}) copy-start(f32[8,8,128,128]{3,2,1,0:T(8,128)} %state_hbm.1) | copy-start | bytes 12582916
  2.8 1.2 %copy-start.1 = (bf16[4096,128]{1,0:T(8,128)(2,1)S(1)}, bf16[4096,128]{1,0:T(8,128)(2,1)}, u32[]{:S(2)}) copy-start(bf16[4096,128]{1,0:T(8,128)(2,1)} %lm_hbm.1) | copy-start | bytes 3145732
  4.1 0.8 %copy-start.2 = (bf16[8,4096]{1,0:T(8,128)(2,1)S(1)}, bf16[8,4096]{1,0:T(8,128)(2,1)}, u32[]{:S(2)}) copy-start(bf16[8,4096]{1,0:T(8,128)(2,1)} %res_hbm.1) | copy-start | bytes 196612
  4.9 0.7 %copy-start.3 = (bf16[8,1024]{1,0:T(8,128)(2,1)S(1)}, bf16[8,1024]{1,0:T(8,128)(2,1)}, u32[]{:S(2)}) copy-start(bf16[8,1024]{1,0:T(8,128)(2,1)} %q_hbm.1) | copy-start | bytes 49156
  5.6 0.7 %copy-start.4 = (bf16[8,1024]{1,0:T(8,128)(2,1)S(1)}, bf16[8,1024]{1,0:T(8,128)(2,1)}, u32[]{:S(2)}) copy-start(bf16[8,1024]{1,0:T(8,128)(2,1)} %k_hbm.1) | copy-start | bytes 49156
  6.3 0.7 %copy-start.5 = (bf16[8,1024]{1,0:T(8,128)(2,1)S(1)}, bf16[8,1024]{1,0:T(8,128)(2,1)}, u32[]{:S(2)}) copy-start(bf16[8,1024]{1,0:T(8,128)(2,1)} %v_hbm.1) | copy-start | bytes 49156
  7.0 0.7 %copy-start.6 = (bf16[8,1024]{1,0:T(8,128)(2,1)S(1)}, bf16[8,1024]{1,0:T(8,128)(2,1)}, u32[]{:S(2)}) copy-start(bf16[8,1024]{1,0:T(8,128)(2,1)} %g_hbm.1) | copy-start | bytes 49156
  7.8 0.7 %copy-start.7 = (f32[4096]{0:T(1024)S(1)}, f32[4096]{0:T(1024)}, u32[]{:S(2)}) copy-start(f32[4096]{0:T(1024)} %param.26) | copy-start | bytes 49156
  8.5 0.7 %copy-start.8 = (f32[4096]{0:T(1024)S(1)}, f32[4096]{0:T(1024)}, u32[]{:S(2)}) copy-start(f32[4096]{0:T(1024)} %param.27) | copy-start | bytes 49156
  9.2 0.7 %copy-start.9 = (f32[8,8]{1,0:T(8,128)S(1)}, f32[8,8]{1,0:T(8,128)}, u32[]{:S(2)}) copy-start(f32[8,8]{1,0:T(8,128)} %dl_hbm.1) | copy-start | bytes 772
  9.9 0.7 %copy-start.10 = (f32[8,8]{1,0:T(8,128)S(1)}, f32[8,8]{1,0:T(8,128)}, u32[]{:S(2)}) copy-start(f32[8,8]{1,0:T(8,128)} %bl_hbm.1) | copy-start | bytes 772
  10.6 0.7 %copy-start.11 = (f32[8]{0:T(128)S(1)}, f32[8]{0:T(128)}, u32[]{:S(2)}) copy-start(f32[8]{0:T(128)} %param.21) | copy-start | bytes 100
  11.2 0.7 %copy-start.12 = (f32[128]{0:T(128)S(1)}, f32[128]{0:T(128)}, u32[]{:S(2)}) copy-start(f32[128]{0:T(128)} %param.23) | copy-start | bytes 1540
  11.9 0.7 %copy-start.13 = (s32[64]{0:T(128)S(1)}, s32[64]{0:T(128)}, u32[]{:S(2)}) copy-start(s32[64]{0:T(128)} %param.29) | copy-start | bytes 772

commit v2 on v1

--- a/solution.py
+++ b/solution.py
@@ -63,7 +63,9 @@
     stat_send,
     stat_recv,
     g_send,
+    z_recv,
     g_recv,
+    p_recv,
     f_send,
     f_recv,
 ):
@@ -73,6 +75,10 @@
     me = my_h * n_b + my_b
     my_y, my_c = my_h // 2, my_h % 2
     n_y = n_h // 2
+    my_z, my_x = my_b // 2, my_b % 2
+    n_z = n_b // 2
+    n_p = n_y * 2
+    upper = my_z * 2 // n_z
     rows, width = q_v.shape
     heads_here = st_v.shape[1]
     size = st_v.shape[2]
@@ -228,30 +234,62 @@
     rstd = 1.0 / jnp.sqrt(total[:, :1] / width_all + epsilon)
     gx_v[me] = (hsum * rstd * gain).astype(bf16)
 
-    def spread(o, carry):
-        other = (me + o) % n_all
-        other_h = other // n_b
+    def forward(slot, other_h, other_b, sem):
         pltpu.make_async_remote_copy(
-            src_ref=gx_v.at[me],
-            dst_ref=gx_v.at[me],
+            src_ref=gx_v.at[slot],
+            dst_ref=gx_v.at[slot],
             send_sem=g_send,
-            recv_sem=g_recv.at[(my_h - other_h + n_h) % n_h],
-            device_id=(other_h, other % n_b),
+            recv_sem=sem,
+            device_id=(other_h, other_b),
             device_id_type=MESH,
         ).start()
-        return carry
-
-    lax.fori_loop(1, n_all, spread, 0)
+
+    def to_partner(slot):
+        forward(slot, my_y * 2 + 1 - my_c, my_b, p_recv)
+
+    def to_plane(slot, z):
+        for o in reversed(range(1, n_p)):
+            other_h = ((my_y + o // 2) % n_y) * 2 + my_c
+            forward(slot, other_h, my_z * 2 + (my_x + o) % 2, g_recv.at[o - 1, z])
+
+    def line(i):
+        base = my_z + upper * (n_z - 1 - 2 * my_z)
+        k = i + (i + n_z - base) // n_z
+        return k + upper * (n_z - 1 - 2 * k)
+
+    for i in reversed(range(n_z - 1)):
+        forward(me, my_h, line(i) * 2 + my_x, z_recv.at[my_z])
+    to_plane(me, my_z)
+    to_partner(me)
 
     value = rstd * total[:, half : half + 1]
     row_of = lax.broadcasted_iota(jnp.int32, ssend_v.shape, 0)
     value_ref[...] = jnp.sum(jnp.where(row_of == lane, value, 0.0), axis=0, keepdims=True)[:, :rows]
 
+    def slab_wait(sem, count):
+        slabs = gx_v.at[pl.ds(0, count)]
+        pltpu.make_async_copy(slabs, slabs, sem).wait()
+
+    for i in range(n_z - 1):
+        z = line(i)
+        slab_wait(z_recv.at[z], 1)
+        slot = my_h * n_b + z * 2 + my_x
+        to_plane(slot, z)
+        to_partner(slot)
+
+    for i in range(n_z):
+        z = line(i - 1) if i else my_z
+        for o in range(1, n_p):
+            slab_wait(g_recv.at[o - 1, z], 1)
+            from_h = ((my_y - o // 2 + n_y) % n_y) * 2 + my_c
+            to_partner(from_h * n_b + z * 2 + (my_x + o) % 2)
+
     logits = None
     for r in range(n_h):
-        other_h = (my_h + r) % n_h
-        arrived = gx_v.at[pl.ds(0, n_b if r else n_b - 1)]
-        pltpu.make_async_copy(arrived, arrived, g_recv.at[r]).wait()
+        if r == n_y:
+            slab_wait(p_recv, n_all // 2)
+        core = my_c if r < n_y else 1 - my_c
+        other_h = ((my_y + r) % n_y) * 2 + core
         block = jnp.concatenate(
             [gx_v[other_h * n_b + b].astype(f32) for b in range(n_b)], axis=0
         ).astype(bf16)
@@ -368,7 +406,9 @@
             pltpu.SemaphoreType.DMA((n_h - 1,)),
             pltpu.SemaphoreType.DMA((n_h - 1,)),
             pltpu.SemaphoreType.DMA,
-            pltpu.SemaphoreType.DMA((n_h,)),
+            pltpu.SemaphoreType.DMA((n_b // 2,)),
+            pltpu.SemaphoreType.DMA((n_h - 1, n_b // 2)),
+            pltpu.SemaphoreType.DMA,
             pltpu.SemaphoreType.DMA,
             pltpu.SemaphoreType.DMA,
         ]
@@ -385,7 +425,7 @@
             ),
             scratch_shapes=scratch,
             compiler_params=pltpu.CompilerParams(
-                collective_id=0, has_side_effects=True, vmem_limit_bytes=48 * 1024 * 1024
+                collective_id=0, has_side_effects=True, vmem_limit_bytes=67043328
             ),
         )(
             queries,

time: 49.6 us -> 33 us (0.67); the launches traced: 48.8 us -> 32.8 us
  local copies, waits for them, and re-layouts: 12.9 us -> 2.25 us
  Pallas kernels: 35.2 us -> 30 us
    unnamed x30 -> x2, local copies, waits for them, and re-layouts: 12.9 us -> 2.25 us
    pallas_call x1, Pallas kernels: 35.2 us -> 30 us  [per_device(): pl.pallas_call(functools.partial(kernel, n_h, n_b), out_shape=(jax.ShapeD...]
where the time goes in v2:
time: 33 us; the launch traced here: 32.8 us
  Pallas kernels  30 us (91%)
  local copies, waits for them, and re-layouts  2.25 us (7%)
  between operations  0.64 us (2%)
    pallas_call x1, Pallas kernels, per_device(): pl.pallas_call(functools.partial(kernel, n_h, n_b), out_shape=(jax.ShapeD...  30 us
    unnamed x2, local copies, waits for them, and re-layouts  2.25 us

profile of v2, /device:TPU:0, one launch (start us, length us, event | category | flops | bytes accessed | tf_op | source)
XLA Modules:
  0.0 32.8 jit_solution(17944630016918734729)
XLA Ops:
  0.6 30.0 %shard_map.158 = (f32[1,8]{1,0:T(1,128)}, f32[1,8]{1,0:T(1,128)}) custom-call(bf16[8,1024]{1,0:T(8,128)(2,1)} %q_hbm.1, bf16[8,1024]{1,0:T(8,128)(2,1)} %k_hbm.1, bf16[8,1024]{1,0:T(8,128)(2,1)} %v_hbm.1, bf16[8,1024]{1,0:T(8,128)(2,1)} %g_hbm.1, f32[8,8]{1,0:T(8,128)} %dl_hbm.1, f32[8,8]{1,0:T(8,128)} %bl_hbm.1, f32[1,8]{1,0:T(1,128)} %bitcast.9, ...), custom_call_target="tpu_custom_call" | custom-call | tf_op jit(solution)/shard_map/pallas_call | solution.py:415
  30.6 1.1 %copy.19 = f32[8]{0:T(128)} copy(f32[8]{0:T(128)} %bitcast.13) | data formatting | bytes 64
  31.7 1.1 %copy.20 = f32[8]{0:T(128)} copy(f32[8]{0:T(128)} %bitcast.12) | data formatting | bytes 64

commit v3 on v2

--- a/solution.py
+++ b/solution.py
@@ -130,14 +130,14 @@
 
     barrier = pltpu.get_barrier_semaphore()
 
-    def greet(o, carry):
-        other = (me + o) % n_all
-        pl.semaphore_signal(
-            barrier, inc=1, device_id=(other // n_b, other % n_b), device_id_type=MESH
-        )
-        return carry
-
-    lax.fori_loop(1, n_all, greet, 0)
+    others = [
+        ((my_h + dh) % n_h, (my_b + db) % n_b)
+        for dh in reversed(range(n_h))
+        for db in reversed(range(n_b))
+        if dh or db
+    ]
+    for other in others:
+        pl.semaphore_signal(barrier, inc=1, device_id=other, device_id_type=MESH)
 
     for copy in loads[:n_early]:
         copy.wait()
@@ -306,19 +306,15 @@
     fx_v[me, 0:1, :batch] = top + jnp.log(mass)
     fx_v[me, 1:2, :batch] = chosen
 
-    def tell(o, carry):
-        other = (me + o) % n_all
+    for other in others:
         pltpu.make_async_remote_copy(
             src_ref=fx_v.at[me],
             dst_ref=fx_v.at[me],
             send_sem=f_send,
             recv_sem=f_recv,
-            device_id=(other // n_b, other % n_b),
+            device_id=other,
             device_id_type=MESH,
         ).start()
-        return carry
-
-    lax.fori_loop(1, n_all, tell, 0)
     arrived = fx_v.at[pl.ds(0, n_all - 1)]
     pltpu.make_async_copy(arrived, arrived, f_recv).wait()
 

time: 33 us -> 32.9 us (level)
  no operation moved by 1% of the time
where the time goes in v3:
time: 32.9 us; the launch traced here: 32.6 us
  Pallas kernels  29.7 us (90%)
  local copies, waits for them, and re-layouts  2.25 us (7%)
  between operations  0.64 us (2%)
    pallas_call x1, Pallas kernels, per_device(): pl.pallas_call(functools.partial(kernel, n_h, n_b), out_shape=(jax.ShapeD...  29.7 us
    unnamed x2, local copies, waits for them, and re-layouts  2.25 us

profile of v3, /device:TPU:0, one launch (start us, length us, event | category | flops | bytes accessed | tf_op | source)
XLA Modules:
  0.0 32.6 jit_solution(3276713395884268560)
XLA Ops:
  0.6 29.7 %shard_map.158 = (f32[1,8]{1,0:T(1,128)}, f32[1,8]{1,0:T(1,128)}) custom-call(bf16[8,1024]{1,0:T(8,128)(2,1)} %q_hbm.1, bf16[8,1024]{1,0:T(8,128)(2,1)} %k_hbm.1, bf16[8,1024]{1,0:T(8,128)(2,1)} %v_hbm.1, bf16[8,1024]{1,0:T(8,128)(2,1)} %g_hbm.1, f32[8,8]{1,0:T(8,128)} %dl_hbm.1, f32[8,8]{1,0:T(8,128)} %bl_hbm.1, f32[1,8]{1,0:T(1,128)} %bitcast.9, ...), custom_call_target="tpu_custom_call" | custom-call | tf_op jit(solution)/shard_map/pallas_call | solution.py:411
  30.4 1.1 %copy.19 = f32[8]{0:T(128)} copy(f32[8]{0:T(128)} %bitcast.13) | data formatting | bytes 64
  31.5 1.1 %copy.20 = f32[8]{0:T(128)} copy(f32[8]{0:T(128)} %bitcast.12) | data formatting | bytes 64
